TPU v7x, 8 devices: a whole 2x2x1 slice. The times are simulated.
8 devices in a mesh: dp: 1 (over z), ep2: 2 (over y), ep: 4 (over x, core).
Axes of the slice: x: 2, y: 2, z: 1, core: 2. Of those that a mesh axis runs over, the one named last changes fastest.
Arguments:
- tokens: bfloat16 [1024, 1536], P(('dp', 'ep2', 'ep'))
- expert_idx: int32 [1024, 8], P(('dp', 'ep2', 'ep'))
- gates: float32 [1024, 8], P(('dp', 'ep2', 'ep'))
- w_gate: bfloat16 [40, 1536, 512], P(('ep2', 'ep'))
- w_up: bfloat16 [40, 1536, 512], P(('ep2', 'ep'))
- w_down: bfloat16 [40, 512, 1536], P(('ep2', 'ep'))
Outputs:
- output: bfloat16 [1024, 1536], P(('dp', 'ep2', 'ep'))
All inputs are finite; a program needn't handle non-finite values.
Results may differ from a plain program's by a relative error of at most 0.001.
Values are sent between devices in bfloat16 or wider.
A program may use at most 1 GiB of HBM per device.

v0:
```python
import jax
import jax.numpy as jnp
from jax import lax
from jax.sharding import PartitionSpec as P


def solution(mesh):
    n_outer = mesh.shape['ep2']
    n_inner = mesh.shape['ep']
    row_spec = P(('dp', 'ep2', 'ep'), None)
    weight_spec = P(('ep2', 'ep'), None, None)

    def local_step(tokens, expert_idx, gates, w_gate, w_up, w_down):
        tok_rows, d_model = tokens.shape
        top_k = expert_idx.shape[1]
        local_exp = w_gate.shape[0]
        n_experts = local_exp * n_outer * n_inner
        capacity = (tok_rows * top_k + n_experts - 1) // n_experts
        n_slots = n_experts * capacity
        flat_ids = expert_idx.reshape(-1)
        one_hot = (flat_ids[:, None] == jnp.arange(n_experts, dtype=jnp.int32)[None, :]).astype(jnp.int32)
        slot_rank = jnp.sum((jnp.cumsum(one_hot, axis=0) - 1) * one_hot, axis=1)
        slot_ids = flat_ids * capacity + slot_rank
        token_of = jnp.arange(tok_rows * top_k, dtype=jnp.int32) // top_k
        source_row = jax.ops.segment_sum(token_of - tok_rows, slot_ids, num_segments=n_slots) + tok_rows
        send_buf = jnp.take(tokens, source_row, axis=0, mode='fill', fill_value=0)
        send_buf = send_buf.reshape(n_outer, n_inner, local_exp, capacity, d_model)
        received = lax.all_to_all(send_buf, 'ep', 1, 1, tiled=True)
        received = lax.all_to_all(received, 'ep2', 0, 0, tiled=True)
        act_gate = jnp.einsum('abecd,edf->abecf', received, w_gate, preferred_element_type=jnp.float32)
        act_up = jnp.einsum('abecd,edf->abecf', received, w_up, preferred_element_type=jnp.float32)
        inner_act = (jax.nn.silu(act_gate) * act_up).astype(jnp.bfloat16)
        expert_out = jnp.einsum('abecf,efd->abecd', inner_act, w_down, preferred_element_type=jnp.float32).astype(jnp.bfloat16)
        returned = lax.all_to_all(expert_out, 'ep2', 0, 0, tiled=True)
        returned = lax.all_to_all(returned, 'ep', 1, 1, tiled=True)
        routed = jnp.take(returned.reshape(n_slots, d_model), slot_ids, axis=0).reshape(tok_rows, top_k, d_model)
        mixed = jnp.sum(gates[:, :, None] * routed, axis=1)
        return (tokens + mixed).astype(jnp.bfloat16)

    return jax.shard_map(local_step, mesh=mesh, in_specs=(row_spec, row_spec, row_spec, weight_spec, weight_spec, weight_spec), out_specs=row_spec, check_vma=False)
```

profile of v0, /device:TPU:0, one launch (start us, length us, event | category | flops | bytes accessed | tf_op | source)
XLA Modules:
  0.0 250.7 jit_solution(15426571000120793817)
XLA Ops:
  0.0 0.8 copy.32
  1.7 11.3 %reduce-window.6 = s32[40,8,128]{2,1,0:T(8,128)S(1)} reduce-window(s32[40,8,128]{2,1,0:T(8,128)S(1)} %fusion.29, s32[]{:T(128)} %constant.53.clone.1), window={size=1x1x128 pad=0_0x0_0x127_0}, to_apply=%region_0.0 | reduce-window | flops 5201920 | bytes 327684 | tf_op jit(solution)/shard_map/reduce-window
  13.7 7.5 %scatter_custom_fusion = s32[1040]{0:T(1024)S(1)} fusion(s32[1024]{0:T(1024)S(1)} %bitcast.71, s32[1024]{0:T(1024)S(1)} %fusion.30, s32[]{:T(128)} %constant.57.clone.1), kind=kCustom, calls=%fused_computation.44 | custom fusion | flops 1024 | bytes 4164 | tf_op jit(solution)/shard_map/scatter-add | solution.py:25
  21.3 5.2 %gather_fusion = bf16[1040,1536]{1,0:T(8,128)(2,1)} fusion(bf16[128,1536]{1,0:T(8,128)(2,1)S(1)} %copy-done, s32[2048]{0:T(1024)S(1)} %pad_clamp_fusion), kind=kCustom, calls=%fused_computation | custom fusion | bytes 6393920 | tf_op jit(solution)/shard_map/jit(_take)/gather | solution.py:26
  26.6 5.5 %gather.13 = bf16[2,4,5,26,1536]{4,3,2,1,0:T(8,128)(2,1)} reshape(bf16[1040,1536]{1,0:T(8,128)(2,1)} %gather_fusion) | data formatting | bytes 6389760 | tf_op jit(solution)/shard_map/jit(_take)/gather | solution.py:26
  32.1 2.5 broadcast_select_fusion
  34.6 3.3 %copy.39 = bf16[2,4,5,26,1536]{4,0,3,2,1:T(2,128)(2,1)S(1)} copy(bf16[2,4,5,26,1536]{4,3,2,1,0:T(8,128)(2,1)S(1)} %broadcast_select_fusion) | data formatting | bytes 6389760 | tf_op jit(solution)/shard_map/jit(_take)/select_n | solution.py:26
  37.9 42.1 %all_to_all.20 = bf16[2,4,5,26,1536]{4,0,3,2,1:T(2,128)(2,1)S(1)} all-to-all(bf16[2,4,5,26,1536]{4,0,3,2,1:T(2,128)(2,1)S(1)} %copy.39), channel_id=1, replica_groups=mesh['dp'=1,'ep2'=2,'ep'=4] {'ep'}, dimensions={1} | all-to-all | bytes 6389760 | tf_op jit(solution)/shard_map/all_to_all | solution.py:28
  80.0 1.2 copy.40
  81.3 39.5 %all_to_all.21 = bf16[2,4,5,26,1536]{4,1,3,2,0:T(4,128)(2,1)S(1)} all-to-all(bf16[2,4,5,26,1536]{4,1,3,2,0:T(4,128)(2,1)S(1)} %copy.40), channel_id=1, replica_groups=mesh['dp'=1,'ep2'=2,'ep'=4] {'ep2'}, dimensions={0} | all-to-all | bytes 6389760 | tf_op jit(solution)/shard_map/all_to_all | solution.py:29
  120.8 1.7 copy-done.1
  122.5 2.2 fusion.4
  124.7 12.9 %fusion.11 = bf16[2,4,5,26,1536]{4,3,1,0,2:T(8,128)(2,1)} fusion(bf16[5,512,1536]{2,1,0:T(8,128)(2,1)} %param.11, f32[5,2,4,26,512]{4,3,2,1,0:T(8,128)S(1)} %fusion.4, bf16[5,1536,512]{2,1,0:T(8,128)(2,1)} %param.10, bf16[2,4,5,26,1536]{4,1,3,2,0:T(4,128)(2,1)} %copy-done.1), kind=kOutput, calls=%fused_computation.14 | convolution fusion | flops 3276349440 | bytes 24248320 | tf_op jit(solution)/shard_map/abecf,efd->abecd/dot_general | solution.py:33
  137.6 4.6 %copy.43 = bf16[2,4,5,26,1536]{4,1,3,2,0:T(4,128)(2,1)S(1)} copy(bf16[2,4,5,26,1536]{4,3,1,0,2:T(8,128)(2,1)} %fusion.11) | data formatting | bytes 6389760 | tf_op jit(solution)/shard_map/convert_element_type | solution.py:33
  142.1 38.7 %all_to_all.22 = bf16[2,4,5,26,1536]{4,1,3,2,0:T(4,128)(2,1)S(1)} all-to-all(bf16[2,4,5,26,1536]{4,1,3,2,0:T(4,128)(2,1)S(1)} %copy.43), channel_id=1, replica_groups=mesh['dp'=1,'ep2'=2,'ep'=4] {'ep2'}, dimensions={0} | all-to-all | bytes 6389760 | tf_op jit(solution)/shard_map/all_to_all | solution.py:34
  180.8 4.1 %copy.44 = bf16[2,4,5,26,1536]{4,0,3,2,1:T(2,128)(2,1)} copy(bf16[2,4,5,26,1536]{4,1,3,2,0:T(4,128)(2,1)S(1)} %all_to_all.22) | data formatting | bytes 6389760 | tf_op jit(solution)/shard_map/all_to_all | solution.py:34
  185.0 5.0 %all-to-all-start.3 = ((bf16[2,4,5,26,1536]{4,0,3,2,1:T(2,128)(2,1)}), bf16[2,4,5,26,1536]{4,0,3,2,1:T(2,128)(2,1)}, u32[]{:S(2)}, u32[]{:S(2)}) async-start(bf16[2,4,5,26,1536]{4,0,3,2,1:T(2,128)(2,1)} %copy.44), calls=%async_computation.3 | async-start | bytes 6389760 | tf_op jit(solution)/shard_map/all_to_all | solution.py:35
  190.3 0.7 copy.31
  191.6 35.3 %all-to-all-done.3 = bf16[2,4,5,26,1536]{4,0,3,2,1:T(2,128)(2,1)} async-done(((bf16[2,4,5,26,1536]{4,0,3,2,1:T(2,128)(2,1)}), bf16[2,4,5,26,1536]{4,0,3,2,1:T(2,128)(2,1)}, u32[]{:S(2)}, u32[]{:S(2)}) %all-to-all-start.3) | async-done | bytes 3194912 | tf_op jit(solution)/shard_map/all_to_all | solution.py:35
  226.9 4.6 %copy.45 = bf16[2,4,5,26,1536]{4,3,2,1,0:T(8,128)(2,1)} copy(bf16[2,4,5,26,1536]{4,0,3,2,1:T(2,128)(2,1)} %all-to-all-done.3) | data formatting | bytes 6389760 | tf_op jit(solution)/shard_map/all_to_all | solution.py:35
  231.5 5.7 %reshape.90 = bf16[1040,1536]{1,0:T(8,128)(2,1)} reshape(bf16[2,4,5,26,1536]{4,3,2,1,0:T(8,128)(2,1)} %copy.45) | data formatting | bytes 6389760 | tf_op jit(solution)/shard_map/reshape | solution.py:36
  237.2 9.1 %gather_fusion.1 = bf16[1024,1536]{1,0:T(8,128)(2,1)S(1)} fusion(bf16[1040,1536]{1,0:T(8,128)(2,1)} %reshape.90, s32[1024]{0:T(1024)} %broadcast_clamp_fusion), kind=kCustom, calls=%fused_computation.1 | custom fusion | bytes 6295552 | tf_op jit(solution)/shard_map/jit(_take)/gather | solution.py:36
  246.3 3.6 %multiply_reduce_fusion = f32[128,1536]{1,0:T(8,128)S(1)} fusion(bf16[1024,1536]{1,0:T(8,128)(2,1)S(1)} %gather_fusion.1, f32[128,8]{1,0:T(8,128)} %copy.31, pred[128,8]{1,0:T(8,128)(4,1)S(1)} %copy.37), kind=kLoop, calls=%fused_computation.9 | loop fusion | flops 6094848 | bytes 3937280 | tf_op jit(solution)/shard_map/reduce_sum | solution.py:37
  249.9 0.8 add_convert_fusion
  (36 shorter events, 2.6 us)
Async XLA Ops:
  0.0 21.3 %copy-start = (bf16[128,1536]{1,0:T(8,128)(2,1)S(1)}, bf16[128,1536]{1,0:T(8,128)(2,1)}, u32[]{:S(2)}) copy-start(bf16[128,1536]{1,0:T(8,128)(2,1)} %param.6) | copy-start | bytes 1179652
  37.9 84.6 %slice-start = ((s8[7864320]{0:T(1024)(128)(4,1)}), s8[4194304]{0:T(1024)(128)(4,1)S(1)}, s32[]{:S(2)}) async-start(s8[7864320]{0:T(1024)(128)(4,1)} %bitcast.72), calls=%async_computation.4 | async-start | bytes 8388608
  80.0 42.5 %slice-start.1 = ((s8[7864320]{0:T(1024)(128)(4,1)}), s8[3670016]{0:T(1024)(128)(4,1)S(1)}, s32[]{:S(2)}) async-start(s8[7864320]{0:T(1024)(128)(4,1)} %bitcast.72), calls=%async_computation.5 | async-start | bytes 7340032
  120.8 1.7 copy-start.1
  185.0 5.2 %copy-start.2 = (s32[128,8]{0,1:T(8,128)S(1)}, s32[128,8]{0,1:T(8,128)}, u32[]{:S(2)}) copy-start(s32[128,8]{0,1:T(8,128)} %param.7) | copy-start | bytes 12292
  185.0 5.3 %copy-start.3 = (f32[128,8]{0,1:T(8,128)S(1)}, f32[128,8]{0,1:T(8,128)}, u32[]{:S(2)}) copy-start(f32[128,8]{0,1:T(8,128)} %param.8) | copy-start | bytes 12292
  185.0 42.0 %all-to-all-start.3 = ((bf16[2,4,5,26,1536]{4,0,3,2,1:T(2,128)(2,1)}), bf16[2,4,5,26,1536]{4,0,3,2,1:T(2,128)(2,1)}, u32[]{:S(2)}, u32[]{:S(2)}) async-start(bf16[2,4,5,26,1536]{4,0,3,2,1:T(2,128)(2,1)} %copy.44), calls=%async_computation.3 | async-start | bytes 6389760 | tf_op jit(solution)/shard_map/all_to_all | solution.py:35
where the time goes:
time: 251 us
  blocking collectives  120 us (48%)
  local copies, waits for them, and re-layouts  47.6 us (19%)
  waiting for transfers between devices  35.3 us (14%)
  other arithmetic  27.2 us (11%)
  matrix products  15.1 us (6%)
  starting transfers between devices  5.01 us (2%)
    all_to_all x1, blocking collectives, local_step(): received = lax.all_to_all(send_buf, 'ep', 1, 1, tiled=True)  42.1 us
    all_to_all x1, blocking collectives, local_step(): received = lax.all_to_all(received, 'ep2', 0, 0, tiled=True)  39.5 us
    all_to_all x1, blocking collectives, local_step(): returned = lax.all_to_all(expert_out, 'ep2', 0, 0, tiled=True)  38.7 us
    all_to_all x1, waiting for transfers between devices, local_step(): returned = lax.all_to_all(returned, 'ep', 1, 1, tiled=True)  35.3 us
    dot_general x1, matrix products, local_step(): jnp.einsum('abecf,efd->abecd', inner_act, w_down, preferred_element_type=...  12.9 us
    another operation x2, other arithmetic  11.3 us
    gather x2, local copies, waits for them, and re-layouts, local_step(): send_buf = jnp.take(tokens, source_row, axis=0, mode='fill', fill_value=0)  10.7 us
    gather x1, local copies, waits for them, and re-layouts, local_step(): jnp.take(returned.reshape(n_slots, d_model), slot_ids, axis=0)  9.1 us
  transfers between devices with their start and end apart: 1, of which 1 were waited for; matrix products, arithmetic and copies ran while one was open for 1% of the time, Pallas kernels for 0%

commit v1 on v0

v1 whole, which is shorter than its diff:
```python
import itertools

import jax
import jax.numpy as jnp
from jax import lax
from jax.experimental import pallas as pl
from jax.experimental.pallas import tpu as pltpu
from jax.sharding import PartitionSpec as P

MESH = pl.DeviceIdType.MESH
F32 = jnp.float32
BF16 = jnp.bfloat16
OWN, XN, YN, DG = 0, 1, 2, 3
SLOT = 32
GROUPS = (((XN, 0), (XN, 1), (YN, 0), (YN, 1)), ((DG, 0), (DG, 1), (OWN, 0), (OWN, 1)))
PIECES = 3


def moe_kernel(
    tok_ref, idx_ref, gate_ref, wg_hbm, wu_hbm, wd_hbm, out_ref,
    wg, wu, wd, toks, idxs, gats, pick, mix, xg, hid, yc, ys, part, relx, rely, finx, finy,
    wsem, ssem, rsem,
):
    n_exp = wg.shape[0]
    rows, d_model = tok_ref.shape
    half = rows // 2
    width = d_model // PIECES
    n_slot = n_exp * SLOT
    top_k = idx_ref.shape[0]

    loads = {}
    wids = itertools.count()
    for name, src, dst in (("g", wg_hbm, wg), ("u", wu_hbm, wu), ("d", wd_hbm, wd)):
        for e in range(n_exp):
            loads[name, e] = pltpu.make_async_copy(src.at[e], dst.at[e], wsem.at[next(wids)])
    for e in range(n_exp):
        loads["g", e].start()
        loads["u", e].start()
    for e in range(n_exp):
        loads["d", e].start()

    iy = lax.axis_index("ep2")
    ie = lax.axis_index("ep")
    ix = ie // 2
    ic = ie % 2
    to_x = {"ep2": iy, "ep": (1 - ix) * 2 + ic}
    to_y = {"ep2": 1 - iy, "ep": ie}
    to_c = {"ep2": iy, "ep": ix * 2 + 1 - ic}
    base_own = (iy * 4 + ie) * n_exp
    base_par = (iy * 4 + ix * 2 + 1 - ic) * n_exp

    barrier = pltpu.get_barrier_semaphore()
    for peer in (to_x, to_y, to_c):
        pl.semaphore_signal(barrier, inc=1, device_id=peer, device_id_type=MESH)
    pl.semaphore_wait(barrier, 3)

    ids = itertools.count()
    sent = []

    def send(src, dst, peer):
        i = next(ids)
        copy = pltpu.make_async_remote_copy(
            src_ref=src, dst_ref=dst, send_sem=ssem.at[i], recv_sem=rsem.at[i],
            device_id=peer, device_id_type=MESH,
        )
        copy.start()
        sent.append(copy)
        return copy

    lo, hi = pl.ds(0, half), pl.ds(half, half)

    def send_route(src_i, src_g, slot, peer):
        return (send(src_i, idxs.at[slot], peer), send(src_g, gats.at[slot], peer))

    def send_rows(src, slot, part_rows, peer):
        return send(src.at[part_rows], toks.at[slot].at[part_rows], peer)

    r_x = send_route(idx_ref, gate_ref, (XN, 0), to_x)
    r_y = send_route(idx_ref, gate_ref, (YN, 0), to_y)
    r_c = send_route(idx_ref, gate_ref, (OWN, 1), to_c)
    t_x0 = send_rows(tok_ref, (XN, 0), lo, to_x)
    t_y1 = send_rows(tok_ref, (YN, 0), hi, to_y)
    t_x1 = send_rows(tok_ref, (XN, 0), hi, to_x)
    t_y0 = send_rows(tok_ref, (YN, 0), lo, to_y)
    t_c = send(tok_ref, toks.at[OWN, 1], to_c)

    def wait_all(copies):
        for copy in copies:
            copy.wait_recv()

    sub16 = lax.broadcasted_iota(jnp.int32, (16, rows), 0)
    exp_id = jnp.where(sub16 < 8, base_own + sub16, base_par + sub16 - 8)
    before = (
        lax.broadcasted_iota(jnp.int32, (rows, rows), 0)
        < lax.broadcasted_iota(jnp.int32, (rows, rows), 1)
    ).astype(F32).astype(BF16)
    place = lax.broadcasted_iota(jnp.int32, (SLOT, rows), 0).astype(F32)

    def prepare(chip, core):
        if (chip, core) == (OWN, 0):
            idx, gat = idx_ref[...], gate_ref[...]
        else:
            idx, gat = idxs[chip, core], gats[chip, core]
        chosen = jnp.zeros((16, rows), F32)
        weight = jnp.zeros((16, rows), F32)
        for j in range(top_k):
            hit = jnp.broadcast_to(idx[j:j + 1, :], (16, rows)) == exp_id
            chosen = jnp.where(hit, 1.0, chosen)
            weight = jnp.where(hit, jnp.broadcast_to(gat[j:j + 1, :], (16, rows)), weight)
        rank = jnp.dot(chosen.astype(BF16), before, preferred_element_type=F32)
        rank = jnp.where(chosen > 0.0, rank, -1.0)
        for e in range(n_exp):
            here = jnp.broadcast_to(rank[e:e + 1, :], (SLOT, rows)) == place
            pick[chip, core, pl.ds(e * SLOT, SLOT), :] = jnp.where(here, 1.0, 0.0).astype(BF16)
        if core == 0:
            cols = []
            for k in range(2 * n_exp):
                row = k if k < n_exp else 8 + k - n_exp
                here = jnp.broadcast_to(rank[row:row + 1, :], (SLOT, rows)) == place
                cols.append(jnp.where(here, jnp.broadcast_to(weight[row:row + 1, :], (SLOT, rows)), 0.0))
            full = jnp.concatenate(cols, axis=0).T
            first = full.astype(BF16)
            rest = full - first.astype(F32)
            second = rest.astype(BF16)
            mix[chip, 0] = first
            mix[chip, 1] = second
            mix[chip, 2] = (rest - second.astype(F32)).astype(BF16)

    def gather(k, chip, core):
        src = tok_ref if (chip, core) == (OWN, 0) else toks.at[chip, core]
        for n in range(PIECES):
            cols = pl.ds(n * width, width)
            got = jnp.dot(pick[chip, core], src[:, cols], preferred_element_type=F32).astype(BF16)
            for e in range(n_exp):
                xg[e, pl.ds(k * SLOT, SLOT), cols] = got[e * SLOT:(e + 1) * SLOT, :]

    def up_gate(e):
        a = jnp.dot(xg[e], wg[e], preferred_element_type=F32)
        b = jnp.dot(xg[e], wu[e], preferred_element_type=F32)
        hid[e] = (jax.nn.silu(a) * b).astype(BF16)

    def down(group, n):
        for e in range(n_exp):
            y = jnp.dot(hid[e], wd[e, :, pl.ds(n * width, width)], preferred_element_type=F32).astype(BF16)
            for k, (chip, core) in enumerate(group):
                piece = y[k * SLOT:(k + 1) * SLOT, :]
                if core == 0:
                    yc[chip, n, pl.ds(e * SLOT, SLOT), :] = piece
                else:
                    ys[chip, n, pl.ds(e * SLOT, SLOT), :] = piece
        return {
            chip: send(ys.at[chip, n], yc.at[chip, n].at[pl.ds(n_slot, n_slot)], to_c)
            for chip, core in group if core == 1
        }

    def combine(chip, n):
        y = yc[chip, n]
        total = jnp.dot(mix[chip, 2], y, preferred_element_type=F32)
        total += jnp.dot(mix[chip, 1], y, preferred_element_type=F32)
        total += jnp.dot(mix[chip, 0], y, preferred_element_type=F32)
        part[chip, n] = total

    prepare(OWN, 0)
    wait_all(r_x)
    r_xc = send_route(idxs.at[XN, 0], gats.at[XN, 0], (XN, 1), to_c)
    r_d = send_route(idxs.at[XN, 0], gats.at[XN, 0], (DG, 0), to_y)
    wait_all(r_y)
    r_yc = send_route(idxs.at[YN, 0], gats.at[YN, 0], (YN, 1), to_c)
    prepare(XN, 0)
    prepare(YN, 0)
    wait_all(r_xc)
    prepare(XN, 1)
    wait_all(r_yc)
    prepare(YN, 1)
    wait_all(r_d)
    r_dc = send_route(idxs.at[DG, 0], gats.at[DG, 0], (DG, 1), to_c)
    prepare(DG, 0)
    wait_all(r_c)
    prepare(OWN, 1)

    t_x0.wait_recv()
    t_d0 = send_rows(toks.at[XN, 0], (DG, 0), lo, to_y)
    t_xc0 = send_rows(toks.at[XN, 0], (XN, 1), lo, to_c)
    t_y1.wait_recv()
    t_d1 = send_rows(toks.at[YN, 0], (DG, 0), hi, to_x)
    t_yc1 = send_rows(toks.at[YN, 0], (YN, 1), hi, to_c)
    wait_all(r_dc)
    prepare(DG, 1)
    t_x1.wait_recv()
    t_xc1 = send_rows(toks.at[XN, 0], (XN, 1), hi, to_c)
    t_y0.wait_recv()
    t_yc0 = send_rows(toks.at[YN, 0], (YN, 1), lo, to_c)

    gather(0, XN, 0)
    gather(2, YN, 0)
    wait_all((t_xc0, t_xc1))
    gather(1, XN, 1)
    wait_all((t_yc0, t_yc1))
    gather(3, YN, 1)
    for e in range(n_exp):
        loads["g", e].wait()
        loads["u", e].wait()
        up_gate(e)
    for e in range(n_exp):
        loads["d", e].wait()

    fin = {}

    def finish_first(n, copies):
        copies[XN].wait_recv()
        combine(XN, n)
        fin["x", 0, n] = send(part.at[XN, n].at[lo], finx.at[n].at[lo], to_x)
        copies[YN].wait_recv()
        combine(YN, n)
        fin["y", 1, n] = send(part.at[YN, n].at[hi], finy.at[n].at[hi], to_y)

    held = down(GROUPS[0], 0)
    for n in range(1, PIECES):
        nxt = down(GROUPS[0], n)
        finish_first(n - 1, held)
        held = nxt
    finish_first(PIECES - 1, held)

    t_d0.wait_recv()
    t_dc0 = send_rows(toks.at[DG, 0], (DG, 1), lo, to_c)
    t_d1.wait_recv()
    t_dc1 = send_rows(toks.at[DG, 0], (DG, 1), hi, to_c)
    gather(2, OWN, 0)
    t_c.wait_recv()
    gather(3, OWN, 1)
    gather(0, DG, 0)
    wait_all((t_dc0, t_dc1))
    gather(1, DG, 1)
    for e in range(n_exp):
        up_gate(e)

    rel = {}
    own_copies = {}

    def finish_second(n, copies):
        copies[DG].wait_recv()
        combine(DG, n)
        rel["x", n] = send(part.at[DG, n].at[lo], relx.at[n], to_x)
        rel["y", n] = send(part.at[DG, n].at[hi], rely.at[n], to_y)
        own_copies[n] = copies[OWN]

    held = down(GROUPS[1], 0)
    for n in range(1, PIECES):
        nxt = down(GROUPS[1], n)
        finish_second(n - 1, held)
        held = nxt
    finish_second(PIECES - 1, held)
    for n in range(PIECES):
        own_copies[n].wait_recv()
        combine(OWN, n)
        part[OWN, n] += tok_ref[:, pl.ds(n * width, width)].astype(F32)

    for n in range(PIECES):
        rel["x", n].wait_recv()
        part[YN, n, lo] += relx[n]
        fin["y", 0, n] = send(part.at[YN, n].at[lo], finy.at[n].at[lo], to_y)
        rel["y", n].wait_recv()
        part[XN, n, hi] += rely[n]
        fin["x", 1, n] = send(part.at[XN, n].at[hi], finx.at[n].at[hi], to_x)

    for n in range(PIECES):
        for a in "xy":
            for s in (0, 1):
                fin[a, s, n].wait_recv()
        out_ref[:, pl.ds(n * width, width)] = (part[OWN, n] + finx[n] + finy[n]).astype(BF16)
    for copy in sent:
        copy.wait_send()


def solution(mesh):
    row_spec = P(('dp', 'ep2', 'ep'), None)
    weight_spec = P(('ep2', 'ep'), None, None)

    def local_step(tokens, expert_idx, gates, w_gate, w_up, w_down):
        rows, d_model = tokens.shape
        top_k = expert_idx.shape[1]
        n_exp, _, d_ff = w_gate.shape
        width = d_model // PIECES
        n_slot = n_exp * SLOT
        vmem = pl.BlockSpec(memory_space=pltpu.VMEM)
        hbm = pl.BlockSpec(memory_space=pl.ANY)
        n_sem = 64
        return pl.pallas_call(
            moe_kernel,
            out_shape=jax.ShapeDtypeStruct((rows, d_model), BF16),
            in_specs=[vmem, vmem, vmem, hbm, hbm, hbm],
            out_specs=vmem,
            scratch_shapes=[
                pltpu.VMEM((n_exp, d_model, d_ff), BF16),
                pltpu.VMEM((n_exp, d_model, d_ff), BF16),
                pltpu.VMEM((n_exp, d_ff, d_model), BF16),
                pltpu.VMEM((4, 2, rows, d_model), BF16),
                pltpu.VMEM((4, 2, top_k, rows), jnp.int32),
                pltpu.VMEM((4, 2, top_k, rows), F32),
                pltpu.VMEM((4, 2, n_slot, rows), BF16),
                pltpu.VMEM((4, 3, rows, 2 * n_slot), BF16),
                pltpu.VMEM((n_exp, 4 * SLOT, d_model), BF16),
                pltpu.VMEM((n_exp, 4 * SLOT, d_ff), BF16),
                pltpu.VMEM((4, PIECES, 2 * n_slot, width), BF16),
                pltpu.VMEM((4, PIECES, n_slot, width), BF16),
                pltpu.VMEM((4, PIECES, rows, width), F32),
                pltpu.VMEM((PIECES, rows // 2, width), F32),
                pltpu.VMEM((PIECES, rows // 2, width), F32),
                pltpu.VMEM((PIECES, rows, width), F32),
                pltpu.VMEM((PIECES, rows, width), F32),
                pltpu.SemaphoreType.DMA((3 * n_exp,)),
                pltpu.SemaphoreType.DMA((n_sem,)),
                pltpu.SemaphoreType.DMA((n_sem,)),
            ],
            compiler_params=pltpu.CompilerParams(
                collective_id=0, has_side_effects=True, vmem_limit_bytes=62 * 1024 * 1024
            ),
            name="moe",
        )(tokens, expert_idx.T, gates.T, w_gate, w_up, w_down)

    return jax.shard_map(
        local_step, mesh=mesh,
        in_specs=(row_spec, row_spec, row_spec, weight_spec, weight_spec, weight_spec),
        out_specs=row_spec, check_vma=False,
    )
```

time: 251 us -> 54.2 us (0.22)
  blocking collectives: 120 us -> 0 us
  Pallas kernels: 0 us -> 52.3 us
  local copies, waits for them, and re-layouts: 47.6 us -> 1.77 us
  waiting for transfers between devices: 35.3 us -> 0 us
  other arithmetic: 27.2 us -> 0 us
  matrix products: 15.1 us -> 0 us
  starting transfers between devices: 5.01 us -> 0 us
    all_to_all x3 -> x0, blocking collectives: 120 us -> none  [the longest x1 42.1 us: local_step(): received = lax.all_to_all(send_buf, 'ep', 1, 1, tiled=True)]
    pallas_call x0 -> x1, Pallas kernels: none -> 52.3 us  [local_step(): pl.pallas_call(moe_kernel, out_shape=jax.ShapeDtypeStruct((rows, d_model)...]
    all_to_all x1 -> x0, waiting for transfers between devices: 35.3 us -> none  [local_step(): returned = lax.all_to_all(returned, 'ep', 1, 1, tiled=True)]
    gather x3 -> x0, local copies, waits for them, and re-layouts: 19.8 us -> none  [the longest x2 10.7 us: local_step(): send_buf = jnp.take(tokens, source_row, axis=0, mode='fill', fill_value=0)]
    dot_general x2 -> x0, matrix products: 15.1 us -> none  [the longest x1 12.9 us: local_step(): jnp.einsum('abecf,efd->abecd', inner_act, w_down, preferred_element_type=...]
    another operation x2 -> x0, other arithmetic: 11.3 us -> none
    all_to_all x3 -> x0, local copies, waits for them, and re-layouts: 9.95 us -> none  [the longest x1 4.59 us: local_step(): returned = lax.all_to_all(returned, 'ep', 1, 1, tiled=True)]
    scatter-add x1 -> x0, other arithmetic: 7.53 us -> none  [local_step(): jax.ops.segment_sum(token_of - tok_rows, slot_ids, num_segments=n_slots)]
  transfers between devices with their start and end apart: 1 -> 0, of which waited for: 1 -> 0; matrix products, arithmetic and copies ran while one was open for 1% -> 0% of each run, Pallas kernels for 0% -> 0%
where the time goes in v1:
time: 54.2 us; the launch traced here: 54.1 us
  Pallas kernels  52.3 us (96%)
  local copies, waits for them, and re-layouts  1.77 us (3%)
    pallas_call x1, Pallas kernels, local_step(): pl.pallas_call(moe_kernel, out_shape=jax.ShapeDtypeStruct((rows, d_model)...  52.3 us
    unnamed x1, local copies, waits for them, and re-layouts  1.77 us

profile of v1, /device:TPU:0, one launch (start us, length us, event | category | flops | bytes accessed | tf_op | source)
XLA Modules:
  0.0 54.1 jit_solution(13417994006640153742)
XLA Ops:
  0.0 52.3 %moe.1 = bf16[128,1536]{1,0:T(8,128)(2,1)} custom-call(bf16[128,1536]{1,0:T(8,128)(2,1)} %tok_ref.1, s32[8,128]{1,0:T(8,128)} %bitcast.2, f32[8,128]{1,0:T(8,128)} %bitcast.3, bf16[5,1536,512]{2,1,0:T(8,128)(2,1)} %wg_hbm.1, bf16[5,1536,512]{2,1,0:T(8,128)(2,1)} %wu_hbm.1, bf16[5,512,1536]{2,1,0:T(8,128)(2,1)} %wd_hbm.1), custom_call_target="tpu_custom_call" | custom-call | tf_op jit(solution)/shard_map/moe/pallas_call | solution.py:288
  52.3 1.8 %copy.8 = bf16[128,1536]{1,0:T(8,128)(2,1)} copy(bf16[128,1536]{1,0:T(8,128)(2,1)} %moe.1) | data formatting | bytes 786432

commit v2 on v1

v2 whole, which is shorter than its diff:
```python
import itertools

import jax
import jax.numpy as jnp
from jax import lax
from jax.experimental import pallas as pl
from jax.experimental.pallas import tpu as pltpu
from jax.sharding import PartitionSpec as P

MESH = pl.DeviceIdType.MESH
F32 = jnp.float32
BF16 = jnp.bfloat16
OWN, XN, YN, DG = 0, 1, 2, 3
SLOT = 32
FIRST = ((XN, 0, 0), (XN, 1, 0), (YN, 0, 1), (YN, 1, 1))
SECOND = ((DG, 0, 0), (DG, 1, 0), (DG, 0, 1), (DG, 1, 1))
THIRD = ((XN, 0, 1), (XN, 1, 1), (YN, 0, 0), (YN, 1, 0))
LAST = ((OWN, 0, 0), (OWN, 1, 0), (OWN, 0, 1), (OWN, 1, 1))
PIECES = 3


def moe_kernel(
    tok_hbm, idx_hbm, gate_hbm, wg_hbm, wu_hbm, wd_hbm, out_ref,
    wg, wu, wd, toks, idxs, gats, pick, mix, xg, hid, yc, ys, part, relx, rely, finx, finy,
    isem, wsem, ssem, rsem,
):
    n_exp = wg.shape[0]
    rows, d_model = out_ref.shape
    half = rows // 2
    width = d_model // PIECES
    n_slot = n_exp * SLOT
    top_k = idx_hbm.shape[0]

    own = [
        pltpu.make_async_copy(idx_hbm, idxs.at[OWN, 0], isem.at[0]),
        pltpu.make_async_copy(gate_hbm, gats.at[OWN, 0], isem.at[1]),
        pltpu.make_async_copy(tok_hbm, toks.at[OWN, 0], isem.at[2]),
    ]
    for copy in own:
        copy.start()

    loads = {}
    wids = itertools.count()
    for name, src, dst in (("g", wg_hbm, wg), ("u", wu_hbm, wu), ("d", wd_hbm, wd)):
        for e in range(n_exp):
            loads[name, e] = pltpu.make_async_copy(src.at[e], dst.at[e], wsem.at[next(wids)])

    iy = lax.axis_index("ep2")
    ie = lax.axis_index("ep")
    ix = ie // 2
    ic = ie % 2
    to_x = {"ep2": iy, "ep": (1 - ix) * 2 + ic}
    to_y = {"ep2": 1 - iy, "ep": ie}
    to_c = {"ep2": iy, "ep": ix * 2 + 1 - ic}
    base_own = (iy * 4 + ie) * n_exp
    base_par = (iy * 4 + ix * 2 + 1 - ic) * n_exp

    barrier = pltpu.get_barrier_semaphore()
    for peer in (to_x, to_y, to_c):
        pl.semaphore_signal(barrier, inc=1, device_id=peer, device_id_type=MESH)
    for e in range(n_exp):
        loads["g", e].start()
        loads["u", e].start()
    for e in range(n_exp):
        loads["d", e].start()
    for copy in own:
        copy.wait()
    pl.semaphore_wait(barrier, 3)

    ids = itertools.count()
    sent = []

    def send(src, dst, peer):
        i = next(ids)
        copy = pltpu.make_async_remote_copy(
            src_ref=src, dst_ref=dst, send_sem=ssem.at[i], recv_sem=rsem.at[i],
            device_id=peer, device_id_type=MESH,
        )
        copy.start()
        sent.append(copy)
        return copy

    halves = (pl.ds(0, half), pl.ds(half, half))

    def send_route(src, dst, peer):
        return (send(idxs.at[src], idxs.at[dst], peer), send(gats.at[src], gats.at[dst], peer))

    def send_rows(src, dst, s, peer):
        return send(toks.at[src].at[halves[s]], toks.at[dst].at[halves[s]], peer)

    def wait_all(copies):
        for copy in copies:
            copy.wait_recv()

    r_x = send_route((OWN, 0), (XN, 0), to_x)
    r_y = send_route((OWN, 0), (YN, 0), to_y)
    r_c = send_route((OWN, 0), (OWN, 1), to_c)
    t_x0 = send_rows((OWN, 0), (XN, 0), 0, to_x)
    t_y1 = send_rows((OWN, 0), (YN, 0), 1, to_y)
    t_x1 = send_rows((OWN, 0), (XN, 0), 1, to_x)
    t_y0 = send_rows((OWN, 0), (YN, 0), 0, to_y)

    sub16 = lax.broadcasted_iota(jnp.int32, (16, rows), 0)
    exp_id = jnp.where(sub16 < 8, base_own + sub16, base_par + sub16 - 8)
    row_i = lax.broadcasted_iota(jnp.int32, (rows, rows), 0)
    col_i = lax.broadcasted_iota(jnp.int32, (rows, rows), 1)
    before = jnp.where((row_i < col_i) & ((row_i < half) == (col_i < half)), 1.0, 0.0).astype(BF16)
    place = lax.broadcasted_iota(jnp.int32, (SLOT, rows), 0).astype(F32)

    def prepare(chip, core):
        idx, gat = idxs[chip, core], gats[chip, core]
        chosen = jnp.zeros((16, rows), F32)
        weight = jnp.zeros((16, rows), F32)
        for j in range(top_k):
            hit = jnp.broadcast_to(idx[j:j + 1, :], (16, rows)) == exp_id
            chosen = jnp.where(hit, 1.0, chosen)
            weight = jnp.where(hit, jnp.broadcast_to(gat[j:j + 1, :], (16, rows)), weight)
        rank = jnp.dot(chosen.astype(BF16), before, preferred_element_type=F32)
        rank = jnp.where(chosen > 0.0, rank, -1.0)
        for s in (0, 1):
            part_rank = rank[:, s * half:(s + 1) * half]
            for e in range(n_exp):
                here = jnp.broadcast_to(part_rank[e:e + 1, :], (SLOT, half)) == place[:, :half]
                pick[chip, core, s, pl.ds(e * SLOT, SLOT), :] = jnp.where(here, 1.0, 0.0).astype(BF16)
        if core == 0:
            cols = []
            for k in range(2 * n_exp):
                row = k if k < n_exp else 8 + k - n_exp
                here = jnp.broadcast_to(rank[row:row + 1, :], (SLOT, rows)) == place
                cols.append(jnp.where(here, jnp.broadcast_to(weight[row:row + 1, :], (SLOT, rows)), 0.0))
            full = jnp.concatenate(cols, axis=0).T
            first = full.astype(BF16)
            rest = full - first.astype(F32)
            second = rest.astype(BF16)
            mix[chip, 0] = first
            mix[chip, 1] = second
            mix[chip, 2] = (rest - second.astype(F32)).astype(BF16)

    def gather(k, chip, core, s):
        for n in range(PIECES):
            cols = pl.ds(n * width, width)
            got = jnp.dot(
                pick[chip, core, s], toks[chip, core, halves[s], cols], preferred_element_type=F32
            ).astype(BF16)
            for e in range(n_exp):
                xg[e, pl.ds(k * SLOT, SLOT), cols] = got[e * SLOT:(e + 1) * SLOT, :]

    def up_gate(e):
        a = jnp.dot(xg[e], wg[e], preferred_element_type=F32)
        b = jnp.dot(xg[e], wu[e], preferred_element_type=F32)
        hid[e] = (jax.nn.silu(a) * b).astype(BF16)

    def down(group, n):
        for e in range(n_exp):
            y = jnp.dot(hid[e], wd[e, :, pl.ds(n * width, width)], preferred_element_type=F32).astype(BF16)
            for k, (chip, core, s) in enumerate(group):
                piece = y[k * SLOT:(k + 1) * SLOT, :]
                dst = ys if core else yc
                dst[chip, s, n, pl.ds(e * SLOT, SLOT), :] = piece
        return [
            send(ys.at[chip, s, n], yc.at[chip, s, n].at[pl.ds(n_slot, n_slot)], to_c)
            for chip, core, s in group if core
        ]

    def combine(chip, s, n):
        y = yc[chip, s, n]
        total = jnp.dot(mix[chip, 2, halves[s]], y, preferred_element_type=F32)
        total += jnp.dot(mix[chip, 1, halves[s]], y, preferred_element_type=F32)
        total += jnp.dot(mix[chip, 0, halves[s]], y, preferred_element_type=F32)
        part[chip, s, n] = total

    def finish(group, after):
        targets = [(chip, s) for chip, core, s in group if core]
        held = down(group, 0)
        for n in range(PIECES):
            nxt = down(group, n + 1) if n + 1 < PIECES else None
            for copy, (chip, s) in zip(held, targets):
                copy.wait_recv()
                combine(chip, s, n)
                after(chip, s, n)
            held = nxt

    fin = {}
    rel = {}

    def send_sum(chip, s, n):
        dst, peer = (finx, to_x) if chip == XN else (finy, to_y)
        fin[chip, s, n] = send(part.at[chip, s, n], dst.at[s, n], peer)

    def send_far(chip, s, n):
        dst, peer = (rely, to_y) if s else (relx, to_x)
        rel[s, n] = send(part.at[chip, s, n], dst.at[n], peer)

    def relay(n):
        for s, chip, src in ((0, YN, relx), (1, XN, rely)):
            rel[s, n].wait_recv()
            part[chip, s, n] += src[n]
            send_sum(chip, s, n)

    def nothing(chip, s, n):
        pass

    wait_all(r_x)
    r_xc = send_route((XN, 0), (XN, 1), to_c)
    r_d = send_route((XN, 0), (DG, 0), to_y)
    wait_all(r_y)
    r_yc = send_route((YN, 0), (YN, 1), to_c)
    prepare(XN, 0)
    prepare(YN, 0)
    wait_all(r_xc)
    prepare(XN, 1)
    wait_all(r_yc)
    prepare(YN, 1)
    wait_all(r_d)
    r_dc = send_route((DG, 0), (DG, 1), to_c)

    t_x0.wait_recv()
    t_d0 = send_rows((XN, 0), (DG, 0), 0, to_y)
    t_xc0 = send_rows((XN, 0), (XN, 1), 0, to_c)
    t_y1.wait_recv()
    t_d1 = send_rows((YN, 0), (DG, 0), 1, to_x)
    t_yc1 = send_rows((YN, 0), (YN, 1), 1, to_c)
    t_c = send(toks.at[OWN, 0], toks.at[OWN, 1], to_c)

    gather(0, *FIRST[0])
    gather(2, *FIRST[2])
    t_xc0.wait_recv()
    gather(1, *FIRST[1])
    t_yc1.wait_recv()
    gather(3, *FIRST[3])
    for e in range(n_exp):
        loads["g", e].wait()
        loads["u", e].wait()
        up_gate(e)
    for e in range(n_exp):
        loads["d", e].wait()
    finish(FIRST, send_sum)

    t_x1.wait_recv()
    t_xc1 = send_rows((XN, 0), (XN, 1), 1, to_c)
    t_y0.wait_recv()
    t_yc0 = send_rows((YN, 0), (YN, 1), 0, to_c)
    prepare(DG, 0)
    wait_all(r_dc)
    prepare(DG, 1)
    t_d0.wait_recv()
    t_dc0 = send_rows((DG, 0), (DG, 1), 0, to_c)
    t_d1.wait_recv()
    t_dc1 = send_rows((DG, 0), (DG, 1), 1, to_c)
    gather(0, *SECOND[0])
    gather(2, *SECOND[2])
    t_dc0.wait_recv()
    gather(1, *SECOND[1])
    t_dc1.wait_recv()
    gather(3, *SECOND[3])
    for e in range(n_exp):
        up_gate(e)
    finish(SECOND, send_far)

    gather(0, *THIRD[0])
    gather(2, *THIRD[2])
    t_xc1.wait_recv()
    gather(1, *THIRD[1])
    t_yc0.wait_recv()
    gather(3, *THIRD[3])
    for e in range(n_exp):
        up_gate(e)
    finish(THIRD, nothing)

    prepare(OWN, 0)
    wait_all(r_c)
    prepare(OWN, 1)
    relay(0)
    t_c.wait_recv()
    for k in range(4):
        gather(k, *LAST[k])
    for e in range(n_exp):
        up_gate(e)
    relay(1)
    finish(LAST, nothing)
    relay(2)

    for n in range(PIECES):
        cols = pl.ds(n * width, width)
        for s in (0, 1):
            part[OWN, s, n] += toks[OWN, 0, halves[s], cols].astype(F32)
    for n in range(PIECES):
        for s in (0, 1):
            fin[XN, s, n].wait_recv()
            fin[YN, s, n].wait_recv()
            out_ref[halves[s], pl.ds(n * width, width)] = (
                part[OWN, s, n] + finx[s, n] + finy[s, n]
            ).astype(BF16)
    for copy in sent:
        copy.wait_send()


def solution(mesh):
    row_spec = P(('dp', 'ep2', 'ep'), None)
    weight_spec = P(('ep2', 'ep'), None, None)

    def local_step(tokens, expert_idx, gates, w_gate, w_up, w_down):
        rows, d_model = tokens.shape
        top_k = expert_idx.shape[1]
        n_exp, _, d_ff = w_gate.shape
        width = d_model // PIECES
        n_slot = n_exp * SLOT
        half = rows // 2
        hbm = pl.BlockSpec(memory_space=pl.ANY)
        n_sem = 80
        args = (tokens, expert_idx.T, gates.T, w_gate, w_up, w_down)
        args = [pltpu.with_memory_space_constraint(a, pltpu.HBM) for a in args]
        return pl.pallas_call(
            moe_kernel,
            out_shape=jax.ShapeDtypeStruct((rows, d_model), BF16),
            in_specs=[hbm] * 6,
            out_specs=pl.BlockSpec(memory_space=pltpu.VMEM),
            scratch_shapes=[
                pltpu.VMEM((n_exp, d_model, d_ff), BF16),
                pltpu.VMEM((n_exp, d_model, d_ff), BF16),
                pltpu.VMEM((n_exp, d_ff, d_model), BF16),
                pltpu.VMEM((4, 2, rows, d_model), BF16),
                pltpu.VMEM((4, 2, top_k, rows), jnp.int32),
                pltpu.VMEM((4, 2, top_k, rows), F32),
                pltpu.VMEM((4, 2, 2, n_slot, half), BF16),
                pltpu.VMEM((4, 3, rows, 2 * n_slot), BF16),
                pltpu.VMEM((n_exp, 4 * SLOT, d_model), BF16),
                pltpu.VMEM((n_exp, 4 * SLOT, d_ff), BF16),
                pltpu.VMEM((4, 2, PIECES, 2 * n_slot, width), BF16),
                pltpu.VMEM((4, 2, PIECES, n_slot, width), BF16),
                pltpu.VMEM((4, 2, PIECES, half, width), F32),
                pltpu.VMEM((PIECES, half, width), F32),
                pltpu.VMEM((PIECES, half, width), F32),
                pltpu.VMEM((2, PIECES, half, width), F32),
                pltpu.VMEM((2, PIECES, half, width), F32),
                pltpu.SemaphoreType.DMA((3,)),
                pltpu.SemaphoreType.DMA((3 * n_exp,)),
                pltpu.SemaphoreType.DMA((n_sem,)),
                pltpu.SemaphoreType.DMA((n_sem,)),
            ],
            compiler_params=pltpu.CompilerParams(
                collective_id=0, has_side_effects=True, vmem_limit_bytes=50 * 1024 * 1024
            ),
            name="moe",
        )(*args)

    return jax.shard_map(
        local_step, mesh=mesh,
        in_specs=(row_spec, row_spec, row_spec, weight_spec, weight_spec, weight_spec),
        out_specs=row_spec, check_vma=False,
    )
```

time: 54.2 us -> 54.4 us (level)
  Pallas kernels: 52.3 us -> 53.6 us
  local copies, waits for them, and re-layouts: 1.77 us -> 0.75 us
    pallas_call x1, Pallas kernels: 52.3 us -> 53.6 us  [local_step(): pl.pallas_call(moe_kernel, out_shape=jax.ShapeDtypeStruct((rows, d_model)...]
    unnamed x1, local copies, waits for them, and re-layouts: 1.77 us -> 0.75 us
where the time goes in v2:
time: 54.4 us; the launch traced here: 54.3 us
  Pallas kernels  53.6 us (99%)
  local copies, waits for them, and re-layouts  0.75 us (1%)
    pallas_call x1, Pallas kernels, local_step(): pl.pallas_call(moe_kernel, out_shape=jax.ShapeDtypeStruct((rows, d_model)...  53.6 us

profile of v2, /device:TPU:0, one launch (start us, length us, event | category | flops | bytes accessed | tf_op | source)
XLA Modules:
  0.0 54.3 jit_solution(3874644982264678079)
XLA Ops:
  0.0 53.6 %moe.1 = bf16[128,1536]{1,0:T(8,128)(2,1)S(1)} custom-call(bf16[128,1536]{1,0:T(8,128)(2,1)} %tok_hbm.1, s32[8,128]{1,0:T(8,128)} %bitcast.2, f32[8,128]{1,0:T(8,128)} %bitcast.3, bf16[5,1536,512]{2,1,0:T(8,128)(2,1)} %wg_hbm.1, bf16[5,1536,512]{2,1,0:T(8,128)(2,1)} %wu_hbm.1, bf16[5,512,1536]{2,1,0:T(8,128)(2,1)} %wd_hbm.1), custom_call_target="tpu_custom_call" | custom-call | tf_op jit(solution)/shard_map/moe/pallas_call | solution.py:313
  53.6 0.7 %copy.8 = bf16[128,1536]{1,0:T(8,128)(2,1)} copy(bf16[128,1536]{1,0:T(8,128)(2,1)S(1)} %moe.1) | data formatting | bytes 786432

commit v3 on v0

v3 whole, which is shorter than its diff:
```python
import itertools

import jax
import jax.numpy as jnp
from jax import lax
from jax.experimental import pallas as pl
from jax.experimental.pallas import tpu as pltpu
from jax.sharding import PartitionSpec as P

MESH = pl.DeviceIdType.MESH
F32 = jnp.float32
BF16 = jnp.bfloat16
OWN, XN, YN, DG = 0, 1, 2, 3
SLOT = 32
UNITS = ((XN, 0, 64), (YN, 64, 64), (DG, 0, 128), (OWN, 0, 128), (XN, 64, 64), (YN, 0, 64))
PIECES = 3


def moe_kernel(
    tok_hbm, idx_hbm, gate_hbm, wg_hbm, wu_hbm, wd_hbm, out_ref,
    wg, wu, wd, toks, idxs, gats, pick, mix, xg, hid, yc, ys, part, relb, finx, finy,
    lsem, ssem, rsem,
):
    n_exp = wg.shape[0]
    rows, d_model = out_ref.shape
    half = rows // 2
    width = d_model // PIECES
    n_slot = n_exp * SLOT
    top_k = idx_hbm.shape[0]

    def at(chip, core):
        return chip * 2 + core

    me = at(OWN, 0)
    own = [
        pltpu.make_async_copy(idx_hbm, idxs.at[me], lsem.at[0]),
        pltpu.make_async_copy(gate_hbm, gats.at[me], lsem.at[1]),
        pltpu.make_async_copy(tok_hbm, toks.at[me], lsem.at[2]),
    ]
    for copy in own:
        copy.start()
    loads = [
        pltpu.make_async_copy(src, dst, lsem.at[3 + i])
        for i, (src, dst) in enumerate(((wg_hbm, wg), (wu_hbm, wu), (wd_hbm, wd)))
    ]

    iy = lax.axis_index("ep2")
    ie = lax.axis_index("ep")
    ix = ie // 2
    ic = ie % 2
    to_x = {"ep2": iy, "ep": (1 - ix) * 2 + ic}
    to_y = {"ep2": 1 - iy, "ep": ie}
    to_c = {"ep2": iy, "ep": ix * 2 + 1 - ic}
    base_own = (iy * 4 + ie) * n_exp
    base_par = (iy * 4 + ix * 2 + 1 - ic) * n_exp

    barrier = pltpu.get_barrier_semaphore()
    for peer in (to_x, to_y, to_c):
        pl.semaphore_signal(barrier, inc=1, device_id=peer, device_id_type=MESH)
    for copy in loads:
        copy.start()
    for copy in own:
        copy.wait()
    pl.semaphore_wait(barrier, 3)

    ids = itertools.count()

    def new_sem():
        return rsem.at[next(ids)]

    def send(src, dst, peer, kind, sem):
        pltpu.make_async_remote_copy(
            src_ref=src, dst_ref=dst, send_sem=ssem.at[kind], recv_sem=sem,
            device_id=peer, device_id_type=MESH,
        ).start()

    def arrived(sem, like):
        pltpu.make_async_copy(like, like, sem).wait()

    def send_route(src, dst, peer):
        sem = new_sem()
        send(idxs.at[src], idxs.at[dst], peer, 0, sem)
        send(gats.at[src], gats.at[dst], peer, 1, sem)
        return lambda: arrived(sem, gats.at[pl.ds(0, 2)])

    def send_rows(src, dst, first, peer, count=half):
        sem = new_sem()
        span = pl.ds(first, count)
        send(toks.at[src].at[span], toks.at[dst].at[span], peer, 2, sem)
        return lambda: arrived(sem, toks.at[dst].at[span])

    r_x = send_route(me, at(XN, 0), to_x)
    r_y = send_route(me, at(YN, 0), to_y)
    r_c = send_route(me, at(OWN, 1), to_c)
    t_x0 = send_rows(me, at(XN, 0), 0, to_x)
    t_y1 = send_rows(me, at(YN, 0), half, to_y)

    sub16 = lax.broadcasted_iota(jnp.int32, (16, rows), 0)
    exp_id = jnp.where(sub16 < 8, base_own + sub16, base_par + sub16 - 8)
    row_i = lax.broadcasted_iota(jnp.int32, (rows, rows), 0)
    col_i = lax.broadcasted_iota(jnp.int32, (rows, rows), 1)
    before = jnp.where(row_i < col_i, 1.0, 0.0).astype(BF16)
    before_half = jnp.where((row_i < col_i) & ((row_i < half) == (col_i < half)), 1.0, 0.0).astype(BF16)
    place = lax.broadcasted_iota(jnp.int32, (SLOT, rows), 0).astype(F32)

    def prepare(chip, core):
        idx, gat = idxs[at(chip, core)], gats[at(chip, core)]
        chosen = jnp.zeros((16, rows), F32)
        weight = jnp.zeros((16, rows), F32)
        for j in range(top_k):
            hit = jnp.broadcast_to(idx[j:j + 1, :], (16, rows)) == exp_id
            chosen = jnp.where(hit, 1.0, chosen)
            weight = jnp.where(hit, jnp.broadcast_to(gat[j:j + 1, :], (16, rows)), weight)
        units = [(u, first, count) for u, (c, first, count) in enumerate(UNITS) if c == chip]
        order = before if len(units) == 1 else before_half
        rank = jnp.dot(chosen.astype(BF16), order, preferred_element_type=F32)
        rank = jnp.where(chosen > 0.0, rank, -1.0)
        for u, first, count in units:
            unit_rank = rank[:, first:first + count]
            for e in range(n_exp):
                here = jnp.broadcast_to(unit_rank[e:e + 1, :], (SLOT, count)) == place[:, :count]
                pick[u, core, pl.ds(e * SLOT, SLOT), pl.ds(0, count)] = jnp.where(here, 1.0, 0.0).astype(BF16)
        if core == 0:
            cols = []
            for k in range(2 * n_exp):
                row = k if k < n_exp else 8 + k - n_exp
                here = jnp.broadcast_to(rank[row:row + 1, :], (SLOT, rows)) == place
                cols.append(jnp.where(here, jnp.broadcast_to(weight[row:row + 1, :], (SLOT, rows)), 0.0))
            full = jnp.concatenate(cols, axis=0).T
            terms = [full.astype(BF16)]
            rest = full - terms[0].astype(F32)
            terms.append(rest.astype(BF16))
            terms.append((rest - terms[1].astype(F32)).astype(BF16))
            for u, first, count in units:
                for t in range(3):
                    mix[u, t, pl.ds(0, count), :] = terms[t][first:first + count, :]

    def gather(k, u, core):
        chip, first, count = UNITS[u]
        for n in range(PIECES):
            cols = pl.ds(n * width, width)
            got = jnp.dot(
                pick[u, core, :, pl.ds(0, count)], toks[at(chip, core), pl.ds(first, count), cols],
                preferred_element_type=F32,
            ).astype(BF16)
            for e in range(n_exp):
                xg[e, pl.ds(k * SLOT, SLOT), cols] = got[e * SLOT:(e + 1) * SLOT, :]

    def up_gate():
        for e in range(n_exp):
            a = jnp.dot(xg[e], wg[e], preferred_element_type=F32)
            b = jnp.dot(xg[e], wu[e], preferred_element_type=F32)
            hid[e] = (jax.nn.silu(a) * b).astype(BF16)

    def down(group, n, sems):
        for e in range(n_exp):
            y = jnp.dot(hid[e], wd[e, :, pl.ds(n * width, width)], preferred_element_type=F32).astype(BF16)
            for k, (u, core) in enumerate(group):
                dst = ys if core else yc
                dst[u, n, pl.ds(e * SLOT, SLOT), :] = y[k * SLOT:(k + 1) * SLOT, :]
        for u, core in group:
            if core:
                send(ys.at[u, n], yc.at[u, n].at[pl.ds(n_slot, n_slot)], to_c, 3, sems[u])

    def combine(u, n):
        chip, first, count = UNITS[u]
        y = yc[u, n]
        total = jnp.dot(mix[u, 2, pl.ds(0, count)], y, preferred_element_type=F32)
        total += jnp.dot(mix[u, 1, pl.ds(0, count)], y, preferred_element_type=F32)
        total += jnp.dot(mix[u, 0, pl.ds(0, count)], y, preferred_element_type=F32)
        for s in (0, 1):
            if first <= s * half < first + count:
                part[chip, s * PIECES + n] = total[s * half - first:(s + 1) * half - first, :]

    def send_sum(chip, s, n, sem):
        dst, peer = (finx, to_x) if chip == XN else (finy, to_y)
        send(part.at[chip, s * PIECES + n], dst.at[s, n], peer, 4, sem)

    r_x()
    r_xc = send_route(at(XN, 0), at(XN, 1), to_c)
    r_d = send_route(at(XN, 0), at(DG, 0), to_y)
    r_y()
    r_yc = send_route(at(YN, 0), at(YN, 1), to_c)
    t_x1 = send_rows(me, at(XN, 0), half, to_x)
    t_y0 = send_rows(me, at(YN, 0), 0, to_y)
    prepare(XN, 0)
    prepare(YN, 0)
    r_xc()
    prepare(XN, 1)
    r_yc()
    prepare(YN, 1)
    prepare(OWN, 0)
    r_c()
    prepare(OWN, 1)

    t_x0()
    t_d0 = send_rows(at(XN, 0), at(DG, 0), 0, to_y)
    t_xc0 = send_rows(at(XN, 0), at(XN, 1), 0, to_c)
    t_y1()
    t_d1 = send_rows(at(YN, 0), at(DG, 0), half, to_x)
    t_yc1 = send_rows(at(YN, 0), at(YN, 1), half, to_c)
    r_d()
    r_dc = send_route(at(DG, 0), at(DG, 1), to_c)
    t_c = send_rows(me, at(OWN, 1), 0, to_c, rows)

    group = ((0, 0), (0, 1), (1, 0), (1, 1))
    gather(0, *group[0])
    gather(2, *group[2])
    prepare(DG, 0)
    t_xc0()
    gather(1, *group[1])
    t_yc1()
    gather(3, *group[3])
    loads[0].wait()
    loads[1].wait()
    up_gate()
    loads[2].wait()
    sems = [new_sem() for _ in range(PIECES)]
    fin_first = new_sem()
    for n in range(PIECES):
        down(group, n, {0: sems[n], 1: sems[n]})
    for n in range(PIECES):
        arrived(sems[n], ys.at[pl.ds(0, 2), n])
        combine(0, n)
        send_sum(XN, 0, n, fin_first)
        combine(1, n)
        send_sum(YN, 1, n, fin_first)

    t_x1()
    t_xc1 = send_rows(at(XN, 0), at(XN, 1), half, to_c)
    t_y0()
    t_yc0 = send_rows(at(YN, 0), at(YN, 1), 0, to_c)
    r_dc()
    prepare(DG, 1)
    group = ((2, 0), (2, 1), (3, 0), (3, 1))
    gather(2, *group[2])
    t_c()
    gather(3, *group[3])
    t_d0()
    t_dc0 = send_rows(at(DG, 0), at(DG, 1), 0, to_c)
    t_d1()
    t_dc1 = send_rows(at(DG, 0), at(DG, 1), half, to_c)
    gather(0, *group[0])
    t_dc0()
    t_dc1()
    gather(1, *group[1])
    up_gate()
    sems = [new_sem() for _ in range(PIECES)]
    own_sem = new_sem()
    far = [new_sem() for _ in range(PIECES)]
    for n in range(PIECES):
        down(group, n, {2: sems[n], 3: own_sem})
    for n in range(PIECES):
        arrived(sems[n], ys.at[2, n])
        combine(2, n)
        send(part.at[DG, n], relb.at[0, n], to_x, 4, far[n])
        send(part.at[DG, PIECES + n], relb.at[1, n], to_y, 4, far[n])

    group = ((4, 0), (4, 1), (5, 0), (5, 1))
    t_xc1()
    t_yc0()
    for k in range(4):
        gather(k, *group[k])
    up_gate()
    sems = [new_sem() for _ in range(PIECES)]
    fin_last = [new_sem() for _ in range(PIECES)]
    for n in range(PIECES):
        down(group, n, {4: sems[n], 5: sems[n]})
    for n in range(PIECES):
        arrived(sems[n], ys.at[pl.ds(4, 2), n])
        combine(4, n)
        combine(5, n)

    for n in range(PIECES):
        arrived(far[n], relb.at[:, n])
        part[YN, n] += relb[0, n]
        send_sum(YN, 0, n, fin_last[n])
        part[XN, PIECES + n] += relb[1, n]
        send_sum(XN, 1, n, fin_last[n])
        if n == 0:
            arrived(own_sem, ys.at[3])
            for m in range(PIECES):
                combine(3, m)
                for s in (0, 1):
                    part[OWN, s * PIECES + m] += toks[
                        me, pl.ds(s * half, half), pl.ds(m * width, width)
                    ].astype(F32)

    arrived(fin_first, finx)
    for n in range(PIECES):
        arrived(fin_last[n], finx.at[:, n])
        for s in (0, 1):
            out_ref[pl.ds(s * half, half), pl.ds(n * width, width)] = (
                part[OWN, s * PIECES + n] + finx[s, n] + finy[s, n]
            ).astype(BF16)
    arrived(ssem.at[0], idxs.at[pl.ds(0, 7)])
    arrived(ssem.at[1], gats.at[pl.ds(0, 7)])
    arrived(ssem.at[2], toks.at[pl.ds(0, 7)])
    arrived(ssem.at[3], ys)
    arrived(ssem.at[4], part.at[pl.ds(0, 3)])


def solution(mesh):
    row_spec = P(('dp', 'ep2', 'ep'), None)
    weight_spec = P(('ep2', 'ep'), None, None)

    def local_step(tokens, expert_idx, gates, w_gate, w_up, w_down):
        rows, d_model = tokens.shape
        top_k = expert_idx.shape[1]
        n_exp, _, d_ff = w_gate.shape
        width = d_model // PIECES
        n_slot = n_exp * SLOT
        half = rows // 2
        hbm = pl.BlockSpec(memory_space=pl.ANY)
        n_sem = 22 + 5 * PIECES
        args = (tokens, expert_idx.T, gates.T, w_gate, w_up, w_down)
        args = [pltpu.with_memory_space_constraint(a, pltpu.HBM) for a in args]
        return pl.pallas_call(
            moe_kernel,
            out_shape=jax.ShapeDtypeStruct((rows, d_model), BF16),
            in_specs=[hbm] * 6,
            out_specs=pl.BlockSpec(memory_space=pltpu.VMEM),
            scratch_shapes=[
                pltpu.VMEM((n_exp, d_model, d_ff), BF16),
                pltpu.VMEM((n_exp, d_model, d_ff), BF16),
                pltpu.VMEM((n_exp, d_ff, d_model), BF16),
                pltpu.VMEM((8, rows, d_model), BF16),
                pltpu.VMEM((8, top_k, rows), jnp.int32),
                pltpu.VMEM((8, top_k, rows), F32),
                pltpu.VMEM((len(UNITS), 2, n_slot, rows), BF16),
                pltpu.VMEM((len(UNITS), 3, rows, 2 * n_slot), BF16),
                pltpu.VMEM((n_exp, 4 * SLOT, d_model), BF16),
                pltpu.VMEM((n_exp, 4 * SLOT, d_ff), BF16),
                pltpu.VMEM((len(UNITS), PIECES, 2 * n_slot, width), BF16),
                pltpu.VMEM((len(UNITS), PIECES, n_slot, width), BF16),
                pltpu.VMEM((4, 2 * PIECES, half, width), F32),
                pltpu.VMEM((2, PIECES, half, width), F32),
                pltpu.VMEM((2, PIECES, half, width), F32),
                pltpu.VMEM((2, PIECES, half, width), F32),
                pltpu.SemaphoreType.DMA((6,)),
                pltpu.SemaphoreType.DMA((5,)),
                pltpu.SemaphoreType.DMA((n_sem,)),
            ],
            compiler_params=pltpu.CompilerParams(
                collective_id=0, has_side_effects=True, vmem_limit_bytes=50 * 1024 * 1024
            ),
            name="moe",
        )(*args)

    return jax.shard_map(
        local_step, mesh=mesh,
        in_specs=(row_spec, row_spec, row_spec, weight_spec, weight_spec, weight_spec),
        out_specs=row_spec, check_vma=False,
    )
```

time: 251 us -> 45.7 us (0.18)
  blocking collectives: 120 us -> 0 us
  local copies, waits for them, and re-layouts: 47.6 us -> 0.75 us
  Pallas kernels: 0 us -> 44.8 us
  waiting for transfers between devices: 35.3 us -> 0 us
  other arithmetic: 27.2 us -> 0 us
  matrix products: 15.1 us -> 0 us
  starting transfers between devices: 5.01 us -> 0 us
    all_to_all x3 -> x0, blocking collectives: 120 us -> none  [the longest x1 42.1 us: local_step(): received = lax.all_to_all(send_buf, 'ep', 1, 1, tiled=True)]
    pallas_call x0 -> x1, Pallas kernels: none -> 44.8 us  [local_step(): pl.pallas_call(moe_kernel, out_shape=jax.ShapeDtypeStruct((rows, d_model)...]
    all_to_all x1 -> x0, waiting for transfers between devices: 35.3 us -> none  [local_step(): returned = lax.all_to_all(returned, 'ep', 1, 1, tiled=True)]
    gather x3 -> x0, local copies, waits for them, and re-layouts: 19.8 us -> none  [the longest x2 10.7 us: local_step(): send_buf = jnp.take(tokens, source_row, axis=0, mode='fill', fill_value=0)]
    dot_general x2 -> x0, matrix products: 15.1 us -> none  [the longest x1 12.9 us: local_step(): jnp.einsum('abecf,efd->abecd', inner_act, w_down, preferred_element_type=...]
    another operation x2 -> x0, other arithmetic: 11.3 us -> none
    all_to_all x3 -> x0, local copies, waits for them, and re-layouts: 9.95 us -> none  [the longest x1 4.59 us: local_step(): returned = lax.all_to_all(returned, 'ep', 1, 1, tiled=True)]
    scatter-add x1 -> x0, other arithmetic: 7.53 us -> none  [local_step(): jax.ops.segment_sum(token_of - tok_rows, slot_ids, num_segments=n_slots)]
  transfers between devices with their start and end apart: 1 -> 0, of which waited for: 1 -> 0; matrix products, arithmetic and copies ran while one was open for 1% -> 0% of each run, Pallas kernels for 0% -> 0%
where the time goes in v3:
time: 45.7 us; the launch traced here: 45.6 us
  Pallas kernels  44.8 us (98%)
  local copies, waits for them, and re-layouts  0.75 us (2%)
    pallas_call x1, Pallas kernels, local_step(): pl.pallas_call(moe_kernel, out_shape=jax.ShapeDtypeStruct((rows, d_model)...  44.8 us

profile of v3, /device:TPU:0, one launch (start us, length us, event | category | flops | bytes accessed | tf_op | source)
XLA Modules:
  0.0 45.6 jit_solution(1299966081363194795)
XLA Ops:
  0.0 44.8 %moe.1 = bf16[128,1536]{1,0:T(8,128)(2,1)S(1)} custom-call(bf16[128,1536]{1,0:T(8,128)(2,1)} %tok_hbm.1, s32[8,128]{1,0:T(8,128)} %bitcast.2, f32[8,128]{1,0:T(8,128)} %bitcast.3, bf16[5,1536,512]{2,1,0:T(8,128)(2,1)} %wg_hbm.1, bf16[5,1536,512]{2,1,0:T(8,128)(2,1)} %wu_hbm.1, bf16[5,512,1536]{2,1,0:T(8,128)(2,1)} %wd_hbm.1), custom_call_target="tpu_custom_call" | custom-call | tf_op jit(solution)/shard_map/moe/pallas_call | solution.py:318
  44.8 0.7 %copy.8 = bf16[128,1536]{1,0:T(8,128)(2,1)} copy(bf16[128,1536]{1,0:T(8,128)(2,1)S(1)} %moe.1) | data formatting | bytes 786432

commit v4 on v3

--- a/solution.py
+++ b/solution.py
@@ -13,7 +13,9 @@
 OWN, XN, YN, DG = 0, 1, 2, 3
 SLOT = 32
 UNITS = ((XN, 0, 64), (YN, 64, 64), (DG, 0, 128), (OWN, 0, 128), (XN, 64, 64), (YN, 0, 64))
+EARLY = 32
 PIECES = 3
+BF16_MAX = float(jnp.finfo(jnp.bfloat16).max)
 
 
 def moe_kernel(
@@ -83,11 +85,14 @@
         send(gats.at[src], gats.at[dst], peer, 1, sem)
         return lambda: arrived(sem, gats.at[pl.ds(0, 2)])
 
+    def start_rows(src, dst, first, count, peer, sem):
+        span = pl.ds(first, count)
+        send(toks.at[src].at[span], toks.at[dst].at[span], peer, 2, sem)
+
     def send_rows(src, dst, first, peer, count=half):
         sem = new_sem()
-        span = pl.ds(first, count)
-        send(toks.at[src].at[span], toks.at[dst].at[span], peer, 2, sem)
-        return lambda: arrived(sem, toks.at[dst].at[span])
+        start_rows(src, dst, first, count, peer, sem)
+        return lambda: arrived(sem, toks.at[dst].at[pl.ds(first, count)])
 
     r_x = send_route(me, at(XN, 0), to_x)
     r_y = send_route(me, at(YN, 0), to_y)
@@ -127,7 +132,7 @@
                 here = jnp.broadcast_to(rank[row:row + 1, :], (SLOT, rows)) == place
                 cols.append(jnp.where(here, jnp.broadcast_to(weight[row:row + 1, :], (SLOT, rows)), 0.0))
             full = jnp.concatenate(cols, axis=0).T
-            terms = [full.astype(BF16)]
+            terms = [jnp.minimum(full, BF16_MAX).astype(BF16)]
             rest = full - terms[0].astype(F32)
             terms.append(rest.astype(BF16))
             terms.append((rest - terms[1].astype(F32)).astype(BF16))
@@ -181,12 +186,13 @@
     r_d = send_route(at(XN, 0), at(DG, 0), to_y)
     r_y()
     r_yc = send_route(at(YN, 0), at(YN, 1), to_c)
-    t_x1 = send_rows(me, at(XN, 0), half, to_x)
-    t_y0 = send_rows(me, at(YN, 0), 0, to_y)
     prepare(XN, 0)
     prepare(YN, 0)
     r_xc()
     prepare(XN, 1)
+    sem_x1, sem_y0 = new_sem(), new_sem()
+    start_rows(me, at(XN, 0), half, EARLY, to_x, sem_x1)
+    start_rows(me, at(YN, 0), 0, EARLY, to_y, sem_y0)
     r_yc()
     prepare(YN, 1)
     prepare(OWN, 0)
@@ -199,6 +205,8 @@
     t_y1()
     t_d1 = send_rows(at(YN, 0), at(DG, 0), half, to_x)
     t_yc1 = send_rows(at(YN, 0), at(YN, 1), half, to_c)
+    start_rows(me, at(XN, 0), half + EARLY, half - EARLY, to_x, sem_x1)
+    start_rows(me, at(YN, 0), EARLY, half - EARLY, to_y, sem_y0)
     r_d()
     r_dc = send_route(at(DG, 0), at(DG, 1), to_c)
     t_c = send_rows(me, at(OWN, 1), 0, to_c, rows)
@@ -226,10 +234,6 @@
         combine(1, n)
         send_sum(YN, 1, n, fin_first)
 
-    t_x1()
-    t_xc1 = send_rows(at(XN, 0), at(XN, 1), half, to_c)
-    t_y0()
-    t_yc0 = send_rows(at(YN, 0), at(YN, 1), 0, to_c)
     r_dc()
     prepare(DG, 1)
     group = ((2, 0), (2, 1), (3, 0), (3, 1))
@@ -245,6 +249,10 @@
     t_dc1()
     gather(1, *group[1])
     up_gate()
+    arrived(sem_x1, toks.at[at(XN, 0)].at[pl.ds(half, half)])
+    t_xc1 = send_rows(at(XN, 0), at(XN, 1), half, to_c)
+    arrived(sem_y0, toks.at[at(YN, 0)].at[pl.ds(0, half)])
+    t_yc0 = send_rows(at(YN, 0), at(YN, 1), 0, to_c)
     sems = [new_sem() for _ in range(PIECES)]
     own_sem = new_sem()
     far = [new_sem() for _ in range(PIECES)]

time: 45.7 us -> 44.9 us (0.982)
  Pallas kernels: 44.8 us -> 44.1 us
    pallas_call x1, Pallas kernels: 44.8 us -> 44.1 us  [local_step(): pl.pallas_call(moe_kernel, out_shape=jax.ShapeDtypeStruct((rows, d_model)...]
where the time goes in v4:
time: 44.9 us; the launch traced here: 44.8 us
  Pallas kernels  44.1 us (98%)
  local copies, waits for them, and re-layouts  0.75 us (2%)
    pallas_call x1, Pallas kernels, local_step(): pl.pallas_call(moe_kernel, out_shape=jax.ShapeDtypeStruct((rows, d_model)...  44.1 us

profile of v4, /device:TPU:0, one launch (start us, length us, event | category | flops | bytes accessed | tf_op | source)
XLA Modules:
  0.0 44.8 jit_solution(13637767898611916400)
XLA Ops:
  0.0 44.1 %moe.1 = bf16[128,1536]{1,0:T(8,128)(2,1)S(1)} custom-call(bf16[128,1536]{1,0:T(8,128)(2,1)} %tok_hbm.1, s32[8,128]{1,0:T(8,128)} %bitcast.2, f32[8,128]{1,0:T(8,128)} %bitcast.3, bf16[5,1536,512]{2,1,0:T(8,128)(2,1)} %wg_hbm.1, bf16[5,1536,512]{2,1,0:T(8,128)(2,1)} %wu_hbm.1, bf16[5,512,1536]{2,1,0:T(8,128)(2,1)} %wd_hbm.1), custom_call_target="tpu_custom_call" | custom-call | tf_op jit(solution)/shard_map/moe/pallas_call | solution.py:326
  44.1 0.7 %copy.8 = bf16[128,1536]{1,0:T(8,128)(2,1)} copy(bf16[128,1536]{1,0:T(8,128)(2,1)S(1)} %moe.1) | data formatting | bytes 786432

commit v5 on v4

--- a/solution.py
+++ b/solution.py
@@ -14,6 +14,7 @@
 SLOT = 32
 UNITS = ((XN, 0, 64), (YN, 64, 64), (DG, 0, 128), (OWN, 0, 128), (XN, 64, 64), (YN, 0, 64))
 EARLY = 32
+LEAD = 16
 PIECES = 3
 BF16_MAX = float(jnp.finfo(jnp.bfloat16).max)
 
@@ -177,9 +178,10 @@
             if first <= s * half < first + count:
                 part[chip, s * PIECES + n] = total[s * half - first:(s + 1) * half - first, :]
 
-    def send_sum(chip, s, n, sem):
+    def send_sum(chip, s, n, sem, first=0, count=half):
         dst, peer = (finx, to_x) if chip == XN else (finy, to_y)
-        send(part.at[chip, s * PIECES + n], dst.at[s, n], peer, 4, sem)
+        span = pl.ds(first, count)
+        send(part.at[chip, s * PIECES + n].at[span], dst.at[s, n].at[span], peer, 4, sem)
 
     r_x()
     r_xc = send_route(at(XN, 0), at(XN, 1), to_c)
@@ -282,9 +284,16 @@
     for n in range(PIECES):
         arrived(far[n], relb.at[:, n])
         part[YN, n] += relb[0, n]
-        send_sum(YN, 0, n, fin_last[n])
         part[XN, PIECES + n] += relb[1, n]
-        send_sum(XN, 1, n, fin_last[n])
+        if n < PIECES - 1:
+            send_sum(YN, 0, n, fin_last[n])
+            send_sum(XN, 1, n, fin_last[n])
+        else:
+            send_sum(YN, 0, n, fin_last[n], 0, LEAD)
+            send_sum(XN, 1, n, fin_last[n], 0, LEAD)
+            pl.when(ic == 1)(lambda: arrived(fin_last[n - 1], finx.at[:, n - 1]))
+            send_sum(YN, 0, n, fin_last[n], LEAD, half - LEAD)
+            send_sum(XN, 1, n, fin_last[n], LEAD, half - LEAD)
         if n == 0:
             arrived(own_sem, ys.at[3])
             for m in range(PIECES):
@@ -296,7 +305,10 @@
 
     arrived(fin_first, finx)
     for n in range(PIECES):
-        arrived(fin_last[n], finx.at[:, n])
+        if n == PIECES - 2:
+            pl.when(ic == 0)(lambda: arrived(fin_last[n], finx.at[:, n]))
+        else:
+            arrived(fin_last[n], finx.at[:, n])
         for s in (0, 1):
             out_ref[pl.ds(s * half, half), pl.ds(n * width, width)] = (
                 part[OWN, s * PIECES + n] + finx[s, n] + finy[s, n]

time: 44.9 us -> 44 us (0.980)
  Pallas kernels: 44.1 us -> 43.1 us
    pallas_call x1, Pallas kernels: 44.1 us -> 43.1 us  [local_step(): pl.pallas_call(moe_kernel, out_shape=jax.ShapeDtypeStruct((rows, d_model)...]
where the time goes in v5:
time: 44 us; the launch traced here: 43.9 us
  Pallas kernels  43.1 us (98%)
  local copies, waits for them, and re-layouts  0.75 us (2%)
    pallas_call x1, Pallas kernels, local_step(): pl.pallas_call(moe_kernel, out_shape=jax.ShapeDtypeStruct((rows, d_model)...  43.1 us

profile of v5, /device:TPU:0, one launch (start us, length us, event | category | flops | bytes accessed | tf_op | source)
XLA Modules:
  0.0 43.9 jit_solution(14915988139226398379)
XLA Ops:
  0.0 43.1 %moe.1 = bf16[128,1536]{1,0:T(8,128)(2,1)S(1)} custom-call(bf16[128,1536]{1,0:T(8,128)(2,1)} %tok_hbm.1, s32[8,128]{1,0:T(8,128)} %bitcast.2, f32[8,128]{1,0:T(8,128)} %bitcast.3, bf16[5,1536,512]{2,1,0:T(8,128)(2,1)} %wg_hbm.1, bf16[5,1536,512]{2,1,0:T(8,128)(2,1)} %wu_hbm.1, bf16[5,512,1536]{2,1,0:T(8,128)(2,1)} %wd_hbm.1), custom_call_target="tpu_custom_call" | custom-call | tf_op jit(solution)/shard_map/moe/pallas_call | solution.py:338
  43.2 0.7 %copy.8 = bf16[128,1536]{1,0:T(8,128)(2,1)} copy(bf16[128,1536]{1,0:T(8,128)(2,1)S(1)} %moe.1) | data formatting | bytes 786432

commit v6 on v5

--- a/solution.py
+++ b/solution.py
@@ -62,8 +62,6 @@
         pl.semaphore_signal(barrier, inc=1, device_id=peer, device_id_type=MESH)
     for copy in loads:
         copy.start()
-    for copy in own:
-        copy.wait()
     pl.semaphore_wait(barrier, 3)
 
     ids = itertools.count()
@@ -82,24 +80,26 @@
 
     def send_route(src, dst, peer):
         sem = new_sem()
-        send(idxs.at[src], idxs.at[dst], peer, 0, sem)
-        send(gats.at[src], gats.at[dst], peer, 1, sem)
+        send(idx_hbm if src is None else idxs.at[src], idxs.at[dst], peer, 0, sem)
+        send(gate_hbm if src is None else gats.at[src], gats.at[dst], peer, 1, sem)
         return lambda: arrived(sem, gats.at[pl.ds(0, 2)])
 
     def start_rows(src, dst, first, count, peer, sem):
         span = pl.ds(first, count)
-        send(toks.at[src].at[span], toks.at[dst].at[span], peer, 2, sem)
+        send((tok_hbm if src is None else toks.at[src]).at[span], toks.at[dst].at[span], peer, 2, sem)
 
     def send_rows(src, dst, first, peer, count=half):
         sem = new_sem()
         start_rows(src, dst, first, count, peer, sem)
         return lambda: arrived(sem, toks.at[dst].at[pl.ds(first, count)])
 
-    r_x = send_route(me, at(XN, 0), to_x)
-    r_y = send_route(me, at(YN, 0), to_y)
-    r_c = send_route(me, at(OWN, 1), to_c)
-    t_x0 = send_rows(me, at(XN, 0), 0, to_x)
-    t_y1 = send_rows(me, at(YN, 0), half, to_y)
+    r_x = send_route(None, at(XN, 0), to_x)
+    r_y = send_route(None, at(YN, 0), to_y)
+    t_x0 = send_rows(None, at(XN, 0), 0, to_x)
+    t_y1 = send_rows(None, at(YN, 0), half, to_y)
+    r_c = send_route(None, at(OWN, 1), to_c)
+    for copy in own:
+        copy.wait()
 
     sub16 = lax.broadcasted_iota(jnp.int32, (16, rows), 0)
     exp_id = jnp.where(sub16 < 8, base_own + sub16, base_par + sub16 - 8)
@@ -185,8 +185,10 @@
 
     r_x()
     r_xc = send_route(at(XN, 0), at(XN, 1), to_c)
-    r_d = send_route(at(XN, 0), at(DG, 0), to_y)
+    d_sem = new_sem()
+    send(idxs.at[at(XN, 0)], idxs.at[at(DG, 0)], to_y, 0, d_sem)
     r_y()
+    send(gats.at[at(YN, 0)], gats.at[at(DG, 0)], to_x, 1, d_sem)
     r_yc = send_route(at(YN, 0), at(YN, 1), to_c)
     prepare(XN, 0)
     prepare(YN, 0)
@@ -209,7 +211,7 @@
     t_yc1 = send_rows(at(YN, 0), at(YN, 1), half, to_c)
     start_rows(me, at(XN, 0), half + EARLY, half - EARLY, to_x, sem_x1)
     start_rows(me, at(YN, 0), EARLY, half - EARLY, to_y, sem_y0)
-    r_d()
+    arrived(d_sem, gats.at[pl.ds(0, 2)])
     r_dc = send_route(at(DG, 0), at(DG, 1), to_c)
     t_c = send_rows(me, at(OWN, 1), 0, to_c, rows)
 
@@ -272,12 +274,12 @@
     for k in range(4):
         gather(k, *group[k])
     up_gate()
-    sems = [new_sem() for _ in range(PIECES)]
+    rest_sem = new_sem()
     fin_last = [new_sem() for _ in range(PIECES)]
     for n in range(PIECES):
-        down(group, n, {4: sems[n], 5: sems[n]})
-    for n in range(PIECES):
-        arrived(sems[n], ys.at[pl.ds(4, 2), n])
+        down(group, n, {4: rest_sem, 5: rest_sem})
+    arrived(rest_sem, ys.at[pl.ds(4, 2)])
+    for n in range(PIECES):
         combine(4, n)
         combine(5, n)
 
@@ -332,7 +334,7 @@
         n_slot = n_exp * SLOT
         half = rows // 2
         hbm = pl.BlockSpec(memory_space=pl.ANY)
-        n_sem = 22 + 5 * PIECES
+        n_sem = 23 + 4 * PIECES
         args = (tokens, expert_idx.T, gates.T, w_gate, w_up, w_down)
         args = [pltpu.with_memory_space_constraint(a, pltpu.HBM) for a in args]
         return pl.pallas_call(

time: 44 us -> 43.9 us (level)
  no operation moved by 1% of the time
where the time goes in v6:
time: 43.9 us; the launch traced here: 43.8 us
  Pallas kernels  43 us (98%)
  local copies, waits for them, and re-layouts  0.75 us (2%)
    pallas_call x1, Pallas kernels, local_step(): pl.pallas_call(moe_kernel, out_shape=jax.ShapeDtypeStruct((rows, d_model)...  43 us

profile of v6, /device:TPU:0, one launch (start us, length us, event | category | flops | bytes accessed | tf_op | source)
XLA Modules:
  0.0 43.8 jit_solution(9639655253235306564)
XLA Ops:
  0.0 43.0 %moe.1 = bf16[128,1536]{1,0:T(8,128)(2,1)S(1)} custom-call(bf16[128,1536]{1,0:T(8,128)(2,1)} %tok_hbm.1, s32[8,128]{1,0:T(8,128)} %bitcast.2, f32[8,128]{1,0:T(8,128)} %bitcast.3, bf16[5,1536,512]{2,1,0:T(8,128)(2,1)} %wg_hbm.1, bf16[5,1536,512]{2,1,0:T(8,128)(2,1)} %wu_hbm.1, bf16[5,512,1536]{2,1,0:T(8,128)(2,1)} %wd_hbm.1), custom_call_target="tpu_custom_call" | custom-call | tf_op jit(solution)/shard_map/moe/pallas_call | solution.py:340
  43.0 0.7 %copy.8 = bf16[128,1536]{1,0:T(8,128)(2,1)} copy(bf16[128,1536]{1,0:T(8,128)(2,1)S(1)} %moe.1) | data formatting | bytes 786432
